TPU v7x, 32 devices: a whole 2x2x4 slice. The times are simulated.
32 devices in a mesh: dp: 4 (over x, core), vocab: 8 (over z, y).
Axes of the slice: x: 2, y: 2, z: 4, core: 2. Of those that a mesh axis runs over, the one named last changes fastest.
Arguments:
- policy_hidden: bfloat16 [512, 4096], P('dp'), may hold values from -84 to 84
- policy_weight: bfloat16 [4096, 65536], P('dp', 'vocab'), may hold values from -0.09375 to 0.09375
- reference_hidden: bfloat16 [512, 4096], P(('dp', 'vocab')), may hold values from -84 to 84
- reference_weight: bfloat16 [4096, 65536], P(None, ('dp', 'vocab')), may hold values from -0.09375 to 0.09375
- targets: int32 [512], replicated, may hold values from 0 to 65535
- response_mask: int32 [512], replicated, may hold values 0 or 1
- pair_index: int32 [16], replicated, may hold values from 0 to 15, each once
Outputs:
- hidden_grad: bfloat16 [512, 4096], P('vocab', 'dp')
- weight_grad: bfloat16 [4096, 65536], P('dp', 'vocab')
- total_loss: float32 [], replicated
Inputs may be any that keep to these rules, and one draw needn't show every extreme that they name: `pair_index`: each number of 0 to 15 once; entries 2p and 2p + 1 are the chosen and the rejected sequence of pair p.
All inputs are finite; a program needn't handle non-finite values.
Results may differ from a plain program's by a relative error of at most 0.005.
The roundings to bfloat16 on the way count: a program that leaves them out, or rounds other values in their place, can miss the bound.
Values may be sent and summed in bfloat16 or wider, within the bound.
A program may use at most 128 MiB of HBM per device.

v0:
```python
import jax
import jax.numpy as jnp
from jax import lax
from jax.sharding import PartitionSpec as P

SEQ_LEN = 32


beta = 0.1
loss_scale = 4096.0


def pair_terms(log_ratio, pair_index):
    chosen = pair_index[0::2]
    rejected = pair_index[1::2]
    margin = beta * (log_ratio[chosen] - log_ratio[rejected])
    pair_count = chosen.shape[0]
    total_loss = jnp.sum(jax.nn.softplus(-margin)) / pair_count
    weight = -beta * loss_scale * jax.nn.sigmoid(-margin) / pair_count
    numbers = jnp.arange(log_ratio.shape[0], dtype=jnp.int32)[:, None]
    factor = jnp.sum(
        jnp.where(numbers == chosen[None, :], weight[None, :], 0.0)
        - jnp.where(numbers == rejected[None, :], weight[None, :], 0.0),
        axis=1,
    )
    return (total_loss, factor)


def local_pick(logits, targets, offset, axis):
    column_ids = lax.broadcasted_iota(jnp.int32, logits.shape, axis)
    shifted = targets - offset
    wanted = shifted[:, None]
    return jnp.sum(jnp.where(column_ids == wanted, logits, 0.0), axis=axis)


def local(
    policy_hidden,
    policy_weight,
    reference_hidden,
    reference_weight,
    targets,
    response_mask,
    pair_index,
):
    data_index = lax.axis_index("dp")
    vocab_index = lax.axis_index("vocab")
    vocab_devices = lax.axis_size("vocab")
    local_tokens = policy_hidden.shape[0]
    policy_width = policy_weight.shape[1]
    reference_width = reference_weight.shape[1]
    active = response_mask.astype(jnp.float32)
    columns = lax.all_to_all(policy_hidden, "dp", split_axis=1, concat_axis=0, tiled=True)
    reference_logits = jnp.dot(
        lax.all_gather(reference_hidden, ("dp", "vocab"), axis=0, tiled=True),
        reference_weight,
        preferred_element_type=jnp.float32,
    )
    reference_offset = (data_index * vocab_devices + vocab_index) * reference_width
    reference_top = jnp.max(reference_logits, axis=1)
    reference_pick = local_pick(reference_logits, targets, reference_offset, 1)
    policy_logits = lax.psum_scatter(
        jnp.dot(columns, policy_weight, preferred_element_type=jnp.float32),
        "dp",
        scatter_dimension=0,
        tiled=True,
    )
    own_targets = lax.dynamic_slice_in_dim(targets, data_index * local_tokens, local_tokens, 0)
    policy_offset = vocab_index * policy_width
    policy_pick = local_pick(policy_logits, own_targets, policy_offset, 1)
    policy_max = lax.pmax(jnp.max(policy_logits, axis=1), "vocab")
    policy_sum, policy_picked = lax.psum(
        (jnp.sum(jnp.exp(policy_logits - policy_max[:, None]), axis=1), policy_pick), "vocab"
    )
    policy_total = policy_max + jnp.log(policy_sum)
    reference_max = lax.pmax(reference_top, ("dp", "vocab"))
    reference_sum, reference_picked = lax.psum(
        (jnp.sum(jnp.exp(reference_logits - reference_max[:, None]), axis=1), reference_pick),
        ("dp", "vocab"),
    )
    reference_logp = reference_picked - reference_max - jnp.log(reference_sum)
    own_reference = lax.dynamic_slice_in_dim(
        reference_logp, data_index * local_tokens, local_tokens, 0
    )
    own_active = lax.dynamic_slice_in_dim(active, data_index * local_tokens, local_tokens, 0)
    own_ratio = jnp.sum(
        (own_active * (policy_picked - policy_total - own_reference)).reshape(-1, SEQ_LEN), axis=1
    )
    log_ratio = lax.all_gather(own_ratio, "dp", axis=0, tiled=True)
    total_loss, factor = pair_terms(log_ratio, pair_index)
    token_scale = lax.dynamic_slice_in_dim(
        active * jnp.repeat(factor, SEQ_LEN), data_index * local_tokens, local_tokens, 0
    )
    column_ids = lax.broadcasted_iota(jnp.int32, policy_logits.shape, 1)
    onehot = (column_ids == (own_targets - policy_offset)[:, None]).astype(jnp.float32)
    logit_grad = (
        token_scale[:, None] * (onehot - jnp.exp(policy_logits - policy_total[:, None]))
    ).astype(jnp.bfloat16)
    segment = lax.all_gather(logit_grad, "dp", axis=0, tiled=True)
    weight_grad = lax.dot_general(
        columns, segment, (((0,), (0,)), ((), ())), preferred_element_type=jnp.float32
    )
    hidden_piece = lax.dot_general(
        segment, policy_weight, (((1,), (1,)), ((), ())), preferred_element_type=jnp.float32
    )
    weight_grad, hidden_part = (weight_grad, hidden_piece)
    hidden_grad = lax.psum_scatter(hidden_part, "vocab", scatter_dimension=0, tiled=True)
    return (hidden_grad.astype(jnp.bfloat16), weight_grad.astype(jnp.bfloat16), total_loss)


def solution(mesh):
    placed = (
        P("dp", None),
        P("dp", "vocab"),
        P(("dp", "vocab"), None),
        P(None, ("dp", "vocab")),
        P(),
        P(),
        P(),
    )
    return jax.shard_map(
        local,
        mesh=mesh,
        in_specs=placed,
        out_specs=(P("vocab", "dp"), P("dp", "vocab"), P()),
        check_vma=False,
    )
```

profile of v0, /device:TPU:0, one launch (start us, length us, event | category | flops | bytes accessed | tf_op | source)
XLA Modules:
  0.0 385.9 jit_solution(17941225385931187928)
XLA Ops:
  8.0 0.0 all-gather.3.cloned.1.call-start
  8.0 0.7 all-gather.3.cloned.1.call-update
  8.7 0.0 reduce-scatter.3.cloned.1.call-start
  8.8 1.6 copy.15
  10.4 19.4 %all_to_all.19 = bf16[128,4,1024]{0,2,1:T(8,128)(2,1)S(1)} all-to-all(bf16[128,4,1024]{0,2,1:T(8,128)(2,1)S(1)} %bitcast.15), channel_id=1, replica_groups=mesh['dp'=4,'vocab'=8] {'dp'}, dimensions={1} | all-to-all | bytes 2097152 | tf_op jit(solution)/shard_map/all_to_all | solution.py:52
  29.8 0.5 copy.16
  30.4 15.8 %fusion.2 = f32[512,8192]{1,0:T(8,128)} fusion(bf16[512,1024]{1,0:T(8,128)(2,1)S(1)} %bitcast.16, bf16[1024,8192]{1,0:T(8,128)(2,1)} %param.8), kind=kOutput, calls=%fused_computation.28 | convolution fusion | flops 8589934592 | bytes 34603008 | tf_op jit(solution)/shard_map/dot_general | solution.py:62
  46.2 0.0 copy-start.2
  46.2 0.0 copy-start
  46.2 0.0 copy-start.3
  46.2 0.0 copy-start.1
  46.2 0.0 reduce-scatter.3.cloned.1.call-update
  46.2 0.0 all-gather.5.cloned.1.call-start
  46.3 0.6 copy-done.2
  46.8 0.1 slice.7
  46.9 0.1 slice.6
  47.0 0.0 copy-done
  47.0 0.0 copy-done.3
  47.1 0.6 dynamic-slice
  48.3 0.0 copy-done.1
  48.3 0.1 dynamic-slice_subtract_fusion
  48.4 28.4 %all-gather.3.cloned.1.call-done = bf16[512,4096]{1,0:T(8,128)(2,1)} async-done(((bf16[16,4096]{1,0:T(8,128)(2,1)}), bf16[512,4096]{1,0:T(8,128)(2,1)}) %all-gather.3.cloned.1.call-update) | async-done | bytes 4194320 | tf_op jit(solution)/shard_map/all_gather | solution.py:54
  76.8 15.7 %fusion.1 = (f32[512]{0:T(512)S(1)}, f32[512,2048]{1,0:T(8,128)}) fusion(bf16[512,4096]{1,0:T(8,128)(2,1)} %all-gather.3.cloned.1.call-done, bf16[4096,2048]{1,0:T(8,128)(2,1)} %param.10), kind=kOutput, calls=%fused_computation.27 | convolution fusion | flops 8590983168 | bytes 25167872 | tf_op jit(solution)/shard_map/dot_general | solution.py:53
  92.5 40.3 %pmax.15 = f32[512]{0:T(512)S(1)} all-reduce(f32[512]{0:T(512)S(1)} %get-tuple-element.27), channel_id=1, replica_groups=mesh['dp'=4,'vocab'=8] {'dp','vocab'}, use_global_device_ids=true, to_apply=%region_10.11 | all-reduce | flops 512 | bytes 4096 | tf_op jit(solution)/shard_map/pmax | solution.py:75
  132.8 3.6 select_reduce_fusion
  136.5 41.4 %all-reduce.1 = (f32[512]{0:T(512)S(1)}, f32[512]{0:T(512)S(1)}) all-reduce(f32[512]{0:T(512)S(1)} %get-tuple-element.18, f32[512]{0:T(512)S(1)} %get-tuple-element.17), channel_id=1, replica_groups=mesh['dp'=4,'vocab'=8] {'dp','vocab'}, use_global_device_ids=true, to_apply=%region_12.13 | all-reduce | flops 1024 | bytes 8192 | tf_op jit(solution)/shard_map/psum | solution.py:76
  177.9 0.0 reduce-scatter.3.cloned.1.call-done
  177.9 2.5 reduce_max.18
  180.3 20.9 %pmax.14 = f32[128]{0:T(128)S(1)} all-reduce(f32[128]{0:T(128)S(1)} %reduce_max.18), channel_id=1, replica_groups=mesh['dp'=4,'vocab'=8] {'vocab'}, use_global_device_ids=true, to_apply=%region_4.5 | all-reduce | flops 128 | bytes 1024 | tf_op jit(solution)/shard_map/pmax | solution.py:70
  201.2 3.4 select_reduce_fusion.1
  204.6 17.1 %all-reduce.2 = (f32[128]{0:T(128)S(1)}, f32[128]{0:T(128)S(1)}) all-reduce(f32[128]{0:T(128)S(1)} %get-tuple-element.16, f32[128]{0:T(128)S(1)} %get-tuple-element.15), channel_id=1, replica_groups=mesh['dp'=4,'vocab'=8] {'vocab'}, use_global_device_ids=true, to_apply=%region_6.7 | all-reduce | flops 256 | bytes 2048 | tf_op jit(solution)/shard_map/psum | solution.py:71
  221.8 0.1 subtract_multiply_fusion.1
  221.8 0.1 reshape.33
  221.9 0.1 reduce_sum.67
  222.1 0.2 dynamic-update-slice
  222.3 5.6 %all-reduce = f32[16]{0:T(128)S(1)} all-reduce(f32[16]{0:T(128)S(1)} %dynamic-update-slice), channel_id=1, replica_groups=mesh['dp'=4,'vocab'=8] {'dp'}, use_global_device_ids=true, to_apply=%add | all-reduce | flops 16 | bytes 128
  227.9 0.6 gather_fusion
  228.6 0.6 gather_fusion.1
  229.2 0.6 fusion
  229.8 0.1 subtract_reduce_fusion
  229.9 0.1 broadcast_in_dim.51
  230.0 0.1 reshape.34
  230.1 0.1 dynamic_slice.15
  230.2 4.7 %multiply_convert_fusion = bf16[128,8192]{1,0:T(8,128)(2,1)} fusion(f32[128,8192]{1,0:T(8,128)} %reduce-scatter.3.cloned.1.call-done, f32[128]{0:T(128)S(1)} %get-tuple-element.24, f32[128]{0:T(128)S(1)} %dynamic_slice.15, s32[128]{0:T(128)S(1)} %dynamic-slice_subtract_fusion), kind=kLoop, calls=%fused_computation.3 | loop fusion | flops 6291456 | bytes 6292992 | tf_op jit(solution)/shard_map/convert_element_type | solution.py:97
  234.9 0.0 all-gather.5.cloned.1.call-update
  234.9 0.0 reduce-scatter.5.cloned.1.call-start
  235.0 56.3 %all-gather.5.cloned.1.call-done = bf16[512,8192]{1,0:T(8,128)(2,1)} async-done(((bf16[128,8192]{1,0:T(8,128)(2,1)}), bf16[512,8192]{1,0:T(8,128)(2,1)}) %all-gather.5.cloned.1.call-update) | async-done | bytes 8388624 | tf_op jit(solution)/shard_map/all_gather | solution.py:98
  291.2 15.9 %fusion.3 = f32[512,1024]{1,0:T(8,128)} fusion(bf16[512,8192]{1,0:T(8,128)(2,1)} %all-gather.5.cloned.1.call-done, bf16[1024,8192]{1,0:T(8,128)(2,1)} %param.8), kind=kOutput, calls=%fused_computation.29 | convolution fusion | flops 8589934592 | bytes 27262976 | tf_op jit(solution)/shard_map/dot_general | solution.py:102
  307.1 0.0 reduce-scatter.5.cloned.1.call-update
  307.8 15.9 %convert_bitcast_fusion = bf16[1024,8192]{0,1:T(8,128)(2,1)} fusion(bf16[512,8192]{1,0:T(8,128)(2,1)} %all-gather.5.cloned.1.call-done, bf16[512,1024]{1,0:T(8,128)(2,1)S(1)} %bitcast.17), kind=kOutput, calls=%fused_computation.2 | convolution fusion | flops 8598323200 | bytes 26214400 | tf_op jit(solution)/shard_map/dot_general | solution.py:99
  323.7 21.3 %copy.17 = bf16[1024,8192]{1,0:T(8,128)(2,1)} copy(bf16[1024,8192]{0,1:T(8,128)(2,1)} %convert_bitcast_fusion) | data formatting | bytes 33554432
  345.0 30.7 %reduce-scatter.5.cloned.1.call-done = f32[64,1024]{1,0:T(8,128)} async-done(((f32[512,1024]{1,0:T(8,128)}), f32[64,1024]{1,0:T(8,128)}) %reduce-scatter.5.cloned.1.call-update) | async-done | bytes 262160 | tf_op jit(solution)/shard_map/reduce_scatter | solution.py:106
  375.8 1.6 convert_element_type.21
  (9 shorter events, 0.0 us)
Async XLA Ops:
  8.0 68.8 %all-gather.3.cloned.1.call-start = ((), (), s32[]{:S(2)}) async-start(), calls=%async_computation.4 | async-start | bytes 4325376 | tf_op jit(solution)/shard_map/all_gather | solution.py:54
  8.7 169.1 %reduce-scatter.3.cloned.1.call-start = ((), (), s32[]{:S(2)}) async-start(), calls=%async_computation.3 | async-start | bytes 20971520 | tf_op jit(solution)/shard_map/reduce_scatter | solution.py:61
  46.2 0.7 copy-start.2
  46.2 0.8 copy-start
  46.2 0.9 copy-start.3
  46.2 2.1 copy-start.1
  46.2 245.0 %all-gather.5.cloned.1.call-start = ((), (), s32[]{:S(2)}) async-start(), calls=%async_computation.5 | async-start | bytes 10485760 | tf_op jit(solution)/shard_map/all_gather | solution.py:98
  234.9 140.8 %reduce-scatter.5.cloned.1.call-start = ((), (), s32[]{:S(2)}) async-start(), calls=%async_computation.6 | async-start | bytes 2359296 | tf_op jit(solution)/shard_map/reduce_scatter | solution.py:106
Sparse Core Ops, SparseCore 0:
  11.9 64.9 all-gather.2
  307.3 68.4 reduce-scatter.4
Sparse Core Ops, SparseCore 1:
  46.3 128.4 reduce-scatter.2
  235.0 56.2 all-gather.4
where the time goes:
time: 387 us; the launch traced here: 386 us
  blocking collectives  145 us (37%)
  waiting for transfers between devices  116 us (30%)
  matrix products  63.3 us (16%)
  local copies, waits for them, and re-layouts  26.6 us (7%)
  between operations  18 us (5%)
  other arithmetic  16.9 us (4%)
    all_gather x1, waiting for transfers between devices, local(): segment = lax.all_gather(logit_grad, 'dp', axis=0, tiled=True)  56.3 us
    psum x1, blocking collectives, local(): lax.psum((jnp.sum(jnp.exp(reference_logits - reference_max[:, None]), axi...  41.4 us
    pmax x1, blocking collectives, local(): reference_max = lax.pmax(reference_top, ('dp', 'vocab'))  40.3 us
    reduce_scatter x1, waiting for transfers between devices, local(): lax.psum_scatter(hidden_part, 'vocab', scatter_dimension=0, tiled=True)  30.7 us
    all_gather x1, waiting for transfers between devices, local(): lax.all_gather(reference_hidden, ('dp', 'vocab'), axis=0, tiled=True)  28.4 us
    unnamed x13, local copies, waits for them, and re-layouts  24.3 us
    pmax x1, blocking collectives, local(): policy_max = lax.pmax(jnp.max(policy_logits, axis=1), 'vocab')  20.9 us
    all_to_all x1, blocking collectives, local(): lax.all_to_all(policy_hidden, 'dp', split_axis=1, concat_axis=0, tiled=True)  19.4 us
  transfers between devices with their start and end apart: 4, of which 3 were waited for; matrix products, arithmetic and copies ran while one was open for 20% of the time, Pallas kernels for 0%

commit v1 on v0

--- a/solution.py
+++ b/solution.py
@@ -1,6 +1,10 @@
+import functools
+
 import jax
 import jax.numpy as jnp
 from jax import lax
+from jax.experimental import pallas as pl
+from jax.experimental.pallas import tpu as pltpu
 from jax.sharding import PartitionSpec as P
 
 SEQ_LEN = 32
@@ -31,6 +35,106 @@
     shifted = targets - offset
     wanted = shifted[:, None]
     return jnp.sum(jnp.where(column_ids == wanted, logits, 0.0), axis=axis)
+
+
+def gather_kernel(nd, nv, x_ref, out_ref, own_sem, send_d, recv_d, send_v, recv_v):
+    d, v = lax.axis_index("dp"), lax.axis_index("vocab")
+    data_peers = [lax.rem(d + k, nd) for k in range(1, nd)]
+    vocab_peers = [lax.rem(v + k, nv) for k in range(1, nv)]
+    barrier = pltpu.get_barrier_semaphore()
+    for peer in data_peers:
+        pl.semaphore_signal(
+            barrier, inc=1, device_id=(peer, v), device_id_type=pl.DeviceIdType.MESH
+        )
+    for peer in vocab_peers:
+        pl.semaphore_signal(
+            barrier, inc=1, device_id=(d, peer), device_id_type=pl.DeviceIdType.MESH
+        )
+    pl.semaphore_wait(barrier, nd + nv - 2)
+    own = pltpu.make_async_copy(x_ref, out_ref.at[v, d], own_sem)
+    own.start()
+    copies = [
+        pltpu.make_async_remote_copy(
+            src_ref=x_ref,
+            dst_ref=out_ref.at[v, d],
+            send_sem=send_d.at[k],
+            recv_sem=recv_d.at[k],
+            device_id=(peer, v),
+            device_id_type=pl.DeviceIdType.MESH,
+        )
+        for k, peer in enumerate(data_peers)
+    ]
+    for copy in copies:
+        copy.start()
+    own.wait()
+    for copy in copies:
+        copy.wait()
+    copies = [
+        pltpu.make_async_remote_copy(
+            src_ref=out_ref.at[v],
+            dst_ref=out_ref.at[v],
+            send_sem=send_v.at[k],
+            recv_sem=recv_v.at[k],
+            device_id=(d, peer),
+            device_id_type=pl.DeviceIdType.MESH,
+        )
+        for k, peer in enumerate(vocab_peers)
+    ]
+    for copy in copies:
+        copy.start()
+    for copy in copies:
+        copy.wait()
+
+
+def gather_stats(stats):
+    nd, nv = lax.axis_size("dp"), lax.axis_size("vocab")
+    size = stats.shape[0]
+    rows = -(-size // 1024) * 8
+    stats = jnp.pad(stats, (0, rows * 128 - size)).reshape(rows, 128)
+    gathered = pl.pallas_call(
+        functools.partial(gather_kernel, nd, nv),
+        out_shape=jax.ShapeDtypeStruct((nv, nd, rows, 128), jnp.float32),
+        in_specs=[pl.BlockSpec(memory_space=pltpu.VMEM)],
+        out_specs=pl.BlockSpec(memory_space=pltpu.VMEM),
+        scratch_shapes=[
+            pltpu.SemaphoreType.DMA,
+            pltpu.SemaphoreType.DMA((nd - 1,)),
+            pltpu.SemaphoreType.DMA((nd - 1,)),
+            pltpu.SemaphoreType.DMA((nv - 1,)),
+            pltpu.SemaphoreType.DMA((nv - 1,)),
+        ],
+        compiler_params=pltpu.CompilerParams(collective_id=0, has_side_effects=True),
+        name="gather_stats",
+    )(stats)
+    return gathered.reshape(nv, nd, rows * 128)[:, :, :size]
+
+
+def grad_kernel(rows_ref, segment_ref, out_ref):
+    out_ref[...] = jnp.dot(
+        rows_ref[...], segment_ref[...], preferred_element_type=jnp.float32
+    ).astype(out_ref.dtype)
+
+
+def grad_matmul(rows, segment):
+    depth, tokens = rows.shape
+    width = segment.shape[1]
+    tile = 512 if width % 512 == 0 else width
+    return pl.pallas_call(
+        grad_kernel,
+        grid=(width // tile,),
+        in_specs=[
+            pl.BlockSpec((depth, tokens), lambda i: (0, 0)),
+            pl.BlockSpec((tokens, tile), lambda i: (0, i)),
+        ],
+        out_specs=pl.BlockSpec((depth, tile), lambda i: (0, i)),
+        out_shape=jax.ShapeDtypeStruct((depth, width), jnp.bfloat16),
+        cost_estimate=pl.CostEstimate(
+            flops=2 * depth * tokens * width,
+            bytes_accessed=2 * (depth * tokens + tokens * width + depth * width),
+            transcendentals=0,
+        ),
+        name="weight_grad",
+    )(rows, segment)
 
 
 def local(
@@ -57,6 +161,7 @@
     )
     reference_offset = (data_index * vocab_devices + vocab_index) * reference_width
     reference_top = jnp.max(reference_logits, axis=1)
+    reference_sum = jnp.sum(jnp.exp(reference_logits - reference_top[:, None]), axis=1)
     reference_pick = local_pick(reference_logits, targets, reference_offset, 1)
     policy_logits = lax.psum_scatter(
         jnp.dot(columns, policy_weight, preferred_element_type=jnp.float32),
@@ -67,28 +172,33 @@
     own_targets = lax.dynamic_slice_in_dim(targets, data_index * local_tokens, local_tokens, 0)
     policy_offset = vocab_index * policy_width
     policy_pick = local_pick(policy_logits, own_targets, policy_offset, 1)
-    policy_max = lax.pmax(jnp.max(policy_logits, axis=1), "vocab")
-    policy_sum, policy_picked = lax.psum(
-        (jnp.sum(jnp.exp(policy_logits - policy_max[:, None]), axis=1), policy_pick), "vocab"
-    )
-    policy_total = policy_max + jnp.log(policy_sum)
-    reference_max = lax.pmax(reference_top, ("dp", "vocab"))
-    reference_sum, reference_picked = lax.psum(
-        (jnp.sum(jnp.exp(reference_logits - reference_max[:, None]), axis=1), reference_pick),
-        ("dp", "vocab"),
-    )
-    reference_logp = reference_picked - reference_max - jnp.log(reference_sum)
-    own_reference = lax.dynamic_slice_in_dim(
-        reference_logp, data_index * local_tokens, local_tokens, 0
-    )
-    own_active = lax.dynamic_slice_in_dim(active, data_index * local_tokens, local_tokens, 0)
-    own_ratio = jnp.sum(
-        (own_active * (policy_picked - policy_total - own_reference)).reshape(-1, SEQ_LEN), axis=1
-    )
-    log_ratio = lax.all_gather(own_ratio, "dp", axis=0, tiled=True)
+    policy_top = jnp.max(policy_logits, axis=1)
+    policy_sum = jnp.sum(jnp.exp(policy_logits - policy_top[:, None]), axis=1)
+    stats = jnp.concatenate(
+        [policy_top, policy_sum, policy_pick, reference_top, reference_sum, reference_pick]
+    )
+    stats = gather_stats(stats)
+    tokens = targets.shape[0]
+    policy_stats = stats[:, :, : 3 * local_tokens].reshape(vocab_devices, -1, 3, local_tokens)
+    policy_max = jnp.max(policy_stats[:, :, 0], axis=0)
+    policy_scaled = policy_stats[:, :, 1] * jnp.exp(policy_stats[:, :, 0] - policy_max[None])
+    policy_totals = (policy_max + jnp.log(jnp.sum(policy_scaled, axis=0))).reshape(tokens)
+    policy_logp = jnp.sum(policy_stats[:, :, 2], axis=0).reshape(tokens) - policy_totals
+    reference_stats = stats[:, :, 3 * local_tokens :].reshape(-1, 3, tokens)
+    reference_max = jnp.max(reference_stats[:, 0], axis=0)
+    reference_scaled = reference_stats[:, 1] * jnp.exp(reference_stats[:, 0] - reference_max[None])
+    reference_logp = (
+        jnp.sum(reference_stats[:, 2], axis=0)
+        - reference_max
+        - jnp.log(jnp.sum(reference_scaled, axis=0))
+    )
+    log_ratio = jnp.sum((active * (policy_logp - reference_logp)).reshape(-1, SEQ_LEN), axis=1)
     total_loss, factor = pair_terms(log_ratio, pair_index)
     token_scale = lax.dynamic_slice_in_dim(
         active * jnp.repeat(factor, SEQ_LEN), data_index * local_tokens, local_tokens, 0
+    )
+    policy_total = lax.dynamic_slice_in_dim(
+        policy_totals, data_index * local_tokens, local_tokens, 0
     )
     column_ids = lax.broadcasted_iota(jnp.int32, policy_logits.shape, 1)
     onehot = (column_ids == (own_targets - policy_offset)[:, None]).astype(jnp.float32)
@@ -96,15 +206,18 @@
         token_scale[:, None] * (onehot - jnp.exp(policy_logits - policy_total[:, None]))
     ).astype(jnp.bfloat16)
     segment = lax.all_gather(logit_grad, "dp", axis=0, tiled=True)
-    weight_grad = lax.dot_general(
-        columns, segment, (((0,), (0,)), ((), ())), preferred_element_type=jnp.float32
-    )
     hidden_piece = lax.dot_general(
         segment, policy_weight, (((1,), (1,)), ((), ())), preferred_element_type=jnp.float32
     )
-    weight_grad, hidden_part = (weight_grad, hidden_piece)
-    hidden_grad = lax.psum_scatter(hidden_part, "vocab", scatter_dimension=0, tiled=True)
-    return (hidden_grad.astype(jnp.bfloat16), weight_grad.astype(jnp.bfloat16), total_loss)
+    pieces = lax.all_to_all(
+        hidden_piece.astype(jnp.bfloat16).reshape(vocab_devices, -1, hidden_piece.shape[1]),
+        "vocab",
+        split_axis=0,
+        concat_axis=0,
+    )
+    hidden_grad = jnp.sum(pieces.astype(jnp.float32), axis=0)
+    weight_grad = grad_matmul(columns.T, segment)
+    return (hidden_grad.astype(jnp.bfloat16), weight_grad, total_loss)
 
 
 def solution(mesh):

time: 387 us -> 319 us (0.82)
  blocking collectives: 145 us -> 19.4 us
  waiting for transfers between devices: 116 us -> 176 us
  Pallas kernels: 0 us -> 32.4 us
  local copies, waits for them, and re-layouts: 26.6 us -> 6.85 us
  matrix products: 63.3 us -> 45.5 us
  starting transfers between devices: 0.17 us -> 5.82 us
    reduce_scatter x1, waiting for transfers between devices: 0.01 us -> 80.1 us  [local(): lax.psum_scatter(jnp.dot(columns, policy_weight, preferred_element_type=j...]
    pmax x2 -> x0, blocking collectives: 61.2 us -> none  [the longest x1 40.3 us: local(): reference_max = lax.pmax(reference_top, ('dp', 'vocab'))]
    psum x2 -> x0, blocking collectives: 58.5 us -> none  [the longest x1 41.4 us: local(): lax.psum((jnp.sum(jnp.exp(reference_logits - reference_max[:, None]), axi...]
    pallas_call x0 -> x2, Pallas kernels: none -> 32.4 us  [the longest x1 19 us: grad_matmul(): pl.pallas_call(grad_kernel, grid=(width // tile,), in_specs=[pl.BlockSpec...]
    reduce_scatter x1 -> x0, waiting for transfers between devices: 30.7 us -> none  [local(): lax.psum_scatter(hidden_part, 'vocab', scatter_dimension=0, tiled=True)]
    unnamed x13 -> x12, local copies, waits for them, and re-layouts: 24.3 us -> 2.04 us
    dot_general x1 -> x0, matrix products: 15.9 us -> none  [local(): lax.dot_general(columns, segment, (((0,), (0,)), ((), ())), preferred_ele...]
    unnamed x1 -> x0, blocking collectives: 5.63 us -> none
  transfers between devices with their start and end apart: 4 -> 4, of which waited for: 3 -> 4; matrix products, arithmetic and copies ran while one was open for 20% -> 11% of each run, Pallas kernels for 0% -> 6%
where the time goes in v1:
time: 319 us; the launch traced here: 318 us
  waiting for transfers between devices  176 us (55%)
  matrix products  45.5 us (14%)
  Pallas kernels  32.4 us (10%)
  blocking collectives  19.4 us (6%)
  between operations  17.5 us (5%)
  other arithmetic  14.1 us (4%)
  local copies, waits for them, and re-layouts  6.85 us (2%)
  starting transfers between devices  5.82 us (2%)
    reduce_scatter x1, waiting for transfers between devices, local(): lax.psum_scatter(jnp.dot(columns, policy_weight, preferred_element_type=j...  80.1 us
    all_gather x1, waiting for transfers between devices, local(): segment = lax.all_gather(logit_grad, 'dp', axis=0, tiled=True)  59.9 us
    all_gather x1, waiting for transfers between devices, local(): lax.all_gather(reference_hidden, ('dp', 'vocab'), axis=0, tiled=True)  30.1 us
    all_to_all x1, blocking collectives, local(): lax.all_to_all(policy_hidden, 'dp', split_axis=1, concat_axis=0, tiled=True)  19.4 us
    pallas_call x1, Pallas kernels, grad_matmul(): pl.pallas_call(grad_kernel, grid=(width // tile,), in_specs=[pl.BlockSpec...  19 us
    dot_general x1, matrix products, local(): jnp.dot(columns, policy_weight, preferred_element_type=jnp.float32)  16 us
    dot_general x1, matrix products, local(): lax.dot_general(segment, policy_weight, (((1,), (1,)), ((), ())), preferr...  15.7 us
    dot_general x1, matrix products, local(): jnp.dot(lax.all_gather(reference_hidden, ('dp', 'vocab'), axis=0, tiled=T...  13.8 us
  transfers between devices with their start and end apart: 4, of which 4 were waited for; matrix products, arithmetic and copies ran while one was open for 11% of the time, Pallas kernels for 6%

profile of v1, /device:TPU:0, one launch (start us, length us, event | category | flops | bytes accessed | tf_op | source)
XLA Modules:
  0.0 317.8 jit_solution(3243412504919556975)
XLA Ops:
  8.0 0.0 all-gather.3.cloned.1.call-start
  8.0 0.7 all-gather.3.cloned.1.call-update
  8.7 0.0 reduce-scatter.2.cloned.1.call-start
  8.8 1.6 copy.22
  10.4 19.4 %all_to_all.24 = bf16[128,4,1024]{0,2,1:T(8,128)(2,1)S(1)} all-to-all(bf16[128,4,1024]{0,2,1:T(8,128)(2,1)S(1)} %bitcast.51), channel_id=1, replica_groups=mesh['dp'=4,'vocab'=8] {'dp'}, dimensions={1} | all-to-all | bytes 2097152 | tf_op jit(solution)/shard_map/all_to_all | solution.py:156
  29.8 16.0 %fusion = f32[512,8192]{1,0:T(8,128)} fusion(bf16[1024,8192]{1,0:T(8,128)(2,1)} %param.8, bf16[128,4,1024]{0,2,1:T(8,128)(2,1)S(1)} %all_to_all.24), kind=kOutput, calls=%fused_computation.11 | convolution fusion | flops 8589934592 | bytes 34603008 | tf_op jit(solution)/shard_map/dot_general | solution.py:167
  45.8 0.0 copy-start.2
  45.8 0.0 copy-start.1
  45.8 0.0 reduce-scatter.2.cloned.1.call-update
  45.8 0.2 all-gather.5.cloned.1.call-start
  46.1 0.4 copy-done.2
  46.5 0.1 slice.35
  46.5 0.1 slice.44
  46.6 0.0 copy-done.1
  46.6 0.1 dynamic-slice_subtract_fusion
  46.8 30.1 %all-gather.3.cloned.1.call-done = bf16[512,4096]{1,0:T(8,128)(2,1)} async-done(((bf16[16,4096]{1,0:T(8,128)(2,1)}), bf16[512,4096]{1,0:T(8,128)(2,1)}) %all-gather.3.cloned.1.call-update) | async-done | bytes 4194320 | tf_op jit(solution)/shard_map/all_gather | solution.py:158
  76.9 13.8 %fusion.11 = (f32[512]{0:T(512)S(1)}, f32[512,2048]{1,0:T(8,128)S(1)}) fusion(bf16[512,4096]{1,0:T(8,128)(2,1)} %all-gather.3.cloned.1.call-done, bf16[4096,2048]{1,0:T(8,128)(2,1)} %param.10), kind=kOutput, calls=%fused_computation.49 | convolution fusion | flops 8590983168 | bytes 25167872 | tf_op jit(solution)/shard_map/dot_general | solution.py:157
  90.7 1.4 select_reduce_fusion
  92.1 80.1 %reduce-scatter.2.cloned.1.call-done = f32[128,8192]{1,0:T(8,128)} async-done(((f32[512,8192]{1,0:T(8,128)}), f32[128,8192]{1,0:T(8,128)}) %reduce-scatter.2.cloned.1.call-update) | async-done | bytes 4194320 | tf_op jit(solution)/shard_map/reduce_scatter | solution.py:166
  172.2 2.5 reduce_max.36
  174.7 0.0 copy-start
  174.7 3.4 %select_reduce_fusion.1 = (f32[128]{0:T(128)S(1)}, f32[128]{0:T(128)S(1)}) fusion(f32[128,8192]{1,0:T(8,128)} %reduce-scatter.2.cloned.1.call-done, s32[128]{0:T(128)S(1)} %dynamic-slice_subtract_fusion, f32[128]{0:T(128)S(1)} %reduce_max.36), kind=kLoop, calls=%fused_computation.6 | loop fusion | flops 5242624 | bytes 4196352 | tf_op jit(solution)/shard_map/reduce_sum | solution.py:37
  178.2 0.6 pad_bitcast_fusion.x_ref
  178.8 13.4 %gather_stats.1 = f32[8,4,16,128]{3,2,1,0:T(8,128)} custom-call(f32[16,128]{1,0:T(8,128)} %pad_bitcast_fusion.x_ref), custom_call_target="tpu_custom_call" | custom-call | tf_op jit(solution)/shard_map/gather_stats/pallas_call | solution.py:94
  192.2 1.0 reshape.59
  193.3 0.1 fusion.10
  193.4 0.2 reshape.62
  193.6 0.2 slice_reduce_fusion
  193.8 0.0 copy-done
  193.8 0.1 reshape.63
  193.9 0.1 reduce_sum.119
  194.0 0.6 gather_fusion
  194.7 0.6 gather_fusion.1
  195.3 0.6 fusion.9
  196.0 0.1 subtract_reduce_fusion
  196.0 0.1 broadcast_in_dim.53
  196.1 0.1 reshape.64
  196.2 0.1 dynamic_slice.10
  196.3 0.1 dynamic_slice.11
  196.4 4.7 %multiply_convert_fusion = bf16[128,8192]{1,0:T(8,128)(2,1)} fusion(f32[128,8192]{1,0:T(8,128)} %reduce-scatter.2.cloned.1.call-done, f32[128]{0:T(128)S(1)} %dynamic_slice.11, f32[128]{0:T(128)S(1)} %dynamic_slice.10, s32[128]{0:T(128)S(1)} %dynamic-slice_subtract_fusion), kind=kLoop, calls=%fused_computation.2 | loop fusion | flops 6291456 | bytes 6292992 | tf_op jit(solution)/shard_map/convert_element_type | solution.py:207
  201.1 0.0 all-gather.5.cloned.1.call-update
  201.1 59.9 %all-gather.5.cloned.1.call-done.segment_ref = bf16[512,8192]{1,0:T(8,128)(2,1)} async-done(((bf16[128,8192]{1,0:T(8,128)(2,1)}), bf16[512,8192]{1,0:T(8,128)(2,1)}) %all-gather.5.cloned.1.call-update) | async-done | bytes 8388624 | tf_op jit(solution)/shard_map/all_gather | solution.py:208
  261.0 15.7 %convolution_convert_fusion = bf16[512,1024]{1,0:T(8,128)(2,1)} fusion(bf16[512,8192]{1,0:T(8,128)(2,1)} %all-gather.5.cloned.1.call-done.segment_ref, bf16[1024,8192]{1,0:T(8,128)(2,1)} %param.8), kind=kOutput, calls=%fused_computation.9 | convolution fusion | flops 8590458880 | bytes 26214400 | tf_op jit(solution)/shard_map/dot_general | solution.py:209
  276.7 5.5 %all-to-all-start.1 = ((bf16[8,64,1024]{2,1,0:T(8,128)(2,1)}), bf16[8,64,1024]{2,1,0:T(8,128)(2,1)S(1)}, u32[]{:S(2)}, u32[]{:S(2)}) async-start(bf16[8,64,1024]{2,1,0:T(8,128)(2,1)} %bitcast.8), calls=%async_computation.2 | async-start | bytes 2097152 | tf_op jit(solution)/shard_map/all_to_all | solution.py:212
  282.2 1.1 bitcast_bitcast_fusion.rows_ref
  284.0 19.0 %weight_grad.1 = bf16[1024,8192]{1,0:T(8,128)(2,1)} custom-call(bf16[1024,512]{1,0:T(8,128)(2,1)} %bitcast_bitcast_fusion.rows_ref, bf16[512,8192]{1,0:T(8,128)(2,1)} %all-gather.5.cloned.1.call-done.segment_ref), custom_call_target="tpu_custom_call" | custom-call | flops 8589934592 | bytes 26214400 | tf_op jit(solution)/shard_map/weight_grad/pallas_call | solution.py:122
  302.9 5.5 %all-to-all-done.1 = bf16[8,64,1024]{2,1,0:T(8,128)(2,1)S(1)} async-done(((bf16[8,64,1024]{2,1,0:T(8,128)(2,1)}), bf16[8,64,1024]{2,1,0:T(8,128)(2,1)S(1)}, u32[]{:S(2)}, u32[]{:S(2)}) %all-to-all-start.1) | async-done | bytes 1048608 | tf_op jit(solution)/shard_map/all_to_all | solution.py:212
  308.4 0.8 reduce_sum.121
  (21 shorter events, 0.2 us)
Async XLA Ops:
  8.0 68.9 %all-gather.3.cloned.1.call-start = ((), (), s32[]{:S(2)}) async-start(), calls=%async_computation.4 | async-start | bytes 4325376 | tf_op jit(solution)/shard_map/all_gather | solution.py:158
  8.7 163.5 %reduce-scatter.2.cloned.1.call-start = ((), (), s32[]{:S(2)}) async-start(), calls=%async_computation.3 | async-start | bytes 20971520 | tf_op jit(solution)/shard_map/reduce_scatter | solution.py:166
  45.8 0.7 copy-start.2
  45.8 0.8 copy-start.1
  45.8 215.2 %all-gather.5.cloned.1.call-start = ((), (), s32[]{:S(2)}) async-start(), calls=%async_computation.5 | async-start | bytes 10485760 | tf_op jit(solution)/shard_map/all_gather | solution.py:208
  174.7 19.1 %copy-start = (s32[512]{0:T(512)S(1)}, s32[512]{0:T(512)}, u32[]{:S(2)}) copy-start(s32[512]{0:T(512)} %param.12) | copy-start | bytes 6148
  276.7 31.7 %all-to-all-start.1 = ((bf16[8,64,1024]{2,1,0:T(8,128)(2,1)}), bf16[8,64,1024]{2,1,0:T(8,128)(2,1)S(1)}, u32[]{:S(2)}, u32[]{:S(2)}) async-start(bf16[8,64,1024]{2,1,0:T(8,128)(2,1)} %bitcast.8), calls=%async_computation.2 | async-start | bytes 2097152 | tf_op jit(solution)/shard_map/all_to_all | solution.py:212
Sparse Core Ops, SparseCore 0:
  11.9 64.9 all-gather.2
Sparse Core Ops, SparseCore 1:
  45.9 126.2 reduce-scatter.1
  201.2 59.8 all-gather.4
